TPU v7x, 32 devices: a whole 2x2x4 slice. The times are simulated.
32 devices in a mesh: rows: 2 (over y), cols: 8 (over z, core), shift: 2 (over x).
Axes of the slice: x: 2, y: 2, z: 4, core: 2. Of those that a mesh axis runs over, the one named last changes fastest.
Arguments:
- train_gate: bfloat16 [7168, 14336], P(('shift', 'rows'), 'cols'), parts along dimension 0, may hold values from -0.09375 to 0.09375
- low_gate: bfloat16 [7168, 64], P(('shift', 'rows')), parts along dimension 0, may hold values from -0.09375 to 0.09375
- high_gate: bfloat16 [128, 14336], P('shift', 'cols'), parts along dimension 0, may hold values from -0.75 to 0.75
- train_up: bfloat16 [7168, 14336], P(('shift', 'rows'), 'cols'), parts along dimension 0, may hold values from -0.09375 to 0.09375
- low_up: bfloat16 [7168, 64], P(('shift', 'rows')), parts along dimension 0, may hold values from -0.09375 to 0.09375
- high_up: bfloat16 [128, 14336], P('shift', 'cols'), parts along dimension 0, may hold values from -0.75 to 0.75
- train_down: bfloat16 [28672, 3584], P(('shift', 'cols'), 'rows'), parts along dimension 0, may hold values from -0.046875 to 0.046875
- low_down: bfloat16 [28672, 64], P(('shift', 'cols')), parts along dimension 0, may hold values from -0.046875 to 0.046875
- high_down: bfloat16 [128, 3584], P('shift', 'rows'), parts along dimension 0, may hold values from -0.75 to 0.75
- norm_train: float32 [7168], P(('shift', 'rows', 'cols')), parts along dimension 0, may hold values from 0.25 to 1.75
- norm_step: float32 [7168], P(('shift', 'rows', 'cols')), parts along dimension 0, may hold values from -0.3 to 0.3
Outputs:
- serving_gate: bfloat16 [28672, 3584], P(('shift', 'cols')), parts along dimension 0
- serving_up: bfloat16 [28672, 3584], P(('shift', 'cols')), parts along dimension 0
- serving_down: bfloat16 [7168, 14336], P('shift', 'cols'), parts along dimension 0
- serve_norm: bfloat16 [7168], P('shift'), parts along dimension 0
There are 2 independent parts, one for each index of `shift`. A program takes and returns all parts, laid end to end along the dimension named above; each array names one. Nothing has to cross between parts.
All inputs are finite; a program needn't handle non-finite values.
Results may differ from a plain program's by a relative error of at most 0.001.
Values may be sent and summed in bfloat16 or wider, within the bound.
A program may use at most 192 MiB of HBM per device.

v0:
```python
import jax
import jax.numpy as jnp
from jax import lax
from jax.sharding import PartitionSpec as P

mix_rate = 1.0


def local(
    train_gate,
    low_gate,
    high_gate,
    train_up,
    low_up,
    high_up,
    train_down,
    low_down,
    high_down,
    norm_train,
    norm_step,
):
    whole_gate = train_gate.astype(jnp.float32) + mix_rate * jnp.dot(
        low_gate, high_gate, preferred_element_type=jnp.float32
    )
    whole_up = train_up.astype(jnp.float32) + mix_rate * jnp.dot(
        low_up, high_up, preferred_element_type=jnp.float32
    )
    whole_down = train_down.astype(jnp.float32) + mix_rate * jnp.dot(
        low_down, high_down, preferred_element_type=jnp.float32
    )
    narrow_gate, narrow_up, narrow_down = (
        whole_gate.astype(jnp.bfloat16),
        whole_up.astype(jnp.bfloat16),
        whole_down.astype(jnp.bfloat16),
    )
    serving_gate, serving_up, serving_down = (
        lax.all_gather(narrow_gate, "rows", axis=0, tiled=True),
        lax.all_gather(narrow_up, "rows", axis=0, tiled=True),
        lax.all_gather(narrow_down, "rows", axis=1, tiled=True),
    )
    serving_gate, serving_up, serving_down = (serving_gate.T, serving_up.T, serving_down.T)
    serve_norm = lax.all_gather(
        (norm_train + norm_step).astype(jnp.bfloat16), ("rows", "cols"), axis=0, tiled=True
    )
    return (serving_gate, serving_up, serving_down, serve_norm)


def solution(mesh):
    return jax.shard_map(
        local,
        mesh=mesh,
        in_specs=(
            P(("shift", "rows"), "cols"),
            P(("shift", "rows"), None),
            P("shift", "cols"),
            P(("shift", "rows"), "cols"),
            P(("shift", "rows"), None),
            P("shift", "cols"),
            P(("shift", "cols"), "rows"),
            P(("shift", "cols"), None),
            P("shift", "rows"),
            P(("shift", "rows", "cols")),
            P(("shift", "rows", "cols")),
        ),
        out_specs=(
            P(("shift", "cols"), None),
            P(("shift", "cols"), None),
            P("shift", "cols"),
            P("shift"),
        ),
        check_vma=False,
    )
```

profile of v0, /device:TPU:0, one launch (start us, length us, event | category | flops | bytes accessed | tf_op | source)
XLA Modules:
  0.0 513.7 jit_solution(3734884600384071257)
XLA Ops:
  7.2 0.0 copy-start
  7.2 0.0 copy-start.2
  7.2 0.0 copy-start.3
  7.2 0.0 all-gather.4.cloned.1.call-start
  7.2 0.9 copy-done
  8.1 7.6 %add_convert_fusion.2 = bf16[1792,1792]{1,0:T(8,128)(2,1)} fusion(bf16[1792,1792]{1,0:T(8,128)(2,1)} %param.11, bf16[1792,64]{0,1:T(8,128)(2,1)S(1)} %copy-done, bf16[64,1792]{1,0:T(8,128)(2,1)} %param.13), kind=kOutput, calls=%fused_computation.2 | convolution fusion | flops 420675584 | bytes 13303808 | tf_op jit(solution)/shard_map/dot_general | solution.py:22
  15.7 0.0 copy-start.4
  15.7 0.0 copy-start.5
  15.7 0.0 all-gather.4.cloned.1.call-update
  15.7 0.0 all-gather.6.cloned.1.call-start
  15.8 0.0 copy-done.2
  15.8 0.0 copy-done.3
  15.8 7.6 %add_convert_fusion.1 = bf16[1792,1792]{1,0:T(8,128)(2,1)} fusion(bf16[1792,1792]{1,0:T(8,128)(2,1)} %param.14, bf16[1792,64]{0,1:T(8,128)(2,1)S(1)} %copy-done.2, bf16[64,1792]{1,0:T(8,128)(2,1)S(1)} %copy-done.3), kind=kOutput, calls=%fused_computation.1 | convolution fusion | flops 420675584 | bytes 13303808 | tf_op jit(solution)/shard_map/dot_general | solution.py:25
  23.4 0.0 copy-start.8
  23.4 0.0 copy-start.6
  23.4 0.0 copy-start.7
  23.4 0.0 all-gather.6.cloned.1.call-update
  23.4 0.0 all-gather.8.cloned.1.call-start
  23.4 0.0 copy-done.4
  23.4 0.0 copy-done.5
  23.5 9.5 %add_convert_fusion = bf16[1792,1792]{1,0:T(8,128)(2,1)} fusion(bf16[1792,1792]{1,0:T(8,128)(2,1)} %param.17, bf16[1792,64]{0,1:T(8,128)(2,1)S(1)} %copy-done.4, bf16[64,1792]{1,0:T(8,128)(2,1)S(1)} %copy-done.5), kind=kOutput, calls=%fused_computation | convolution fusion | flops 420675584 | bytes 13303808 | tf_op jit(solution)/shard_map/dot_general | solution.py:28
  32.9 0.0 all-gather.8.cloned.1.call-update
  33.0 0.0 copy-done.8
  33.0 0.6 dynamic-slice
  34.2 0.0 copy-done.6
  34.2 0.0 copy-done.7
  34.3 0.2 dynamic-update-slice
  34.5 36.7 %all-reduce = bf16[3584]{0:T(1024)(128)(2,1)} all-reduce(bf16[3584]{0:T(1024)(128)(2,1)S(1)} %dynamic-update-slice), channel_id=1, replica_groups=mesh['rows'=2,'cols'=8,'shift'=2] {'rows','cols'}, use_global_device_ids=true, to_apply=%add | all-reduce | flops 3584 | bytes 14336
  71.2 103.5 %all-gather.4.cloned.1.call-done = bf16[3584,1792]{1,0:T(8,128)(2,1)} async-done(((bf16[1792,1792]{1,0:T(8,128)(2,1)}), bf16[3584,1792]{1,0:T(8,128)(2,1)}) %all-gather.4.cloned.1.call-update) | async-done | bytes 12845072 | tf_op jit(solution)/shard_map/all_gather | solution.py:37
  174.7 19.0 %copy.15 = bf16[1792,3584]{1,0:T(8,128)(2,1)} copy(bf16[1792,3584]{0,1:T(8,128)(2,1)} %bitcast.10) | data formatting | bytes 25690112
  193.6 138.5 %all-gather.6.cloned.1.call-done = bf16[3584,1792]{1,0:T(8,128)(2,1)} async-done(((bf16[1792,1792]{1,0:T(8,128)(2,1)}), bf16[3584,1792]{1,0:T(8,128)(2,1)}) %all-gather.6.cloned.1.call-update) | async-done | bytes 12845072 | tf_op jit(solution)/shard_map/all_gather | solution.py:38
  332.1 19.0 %copy.16 = bf16[1792,3584]{1,0:T(8,128)(2,1)} copy(bf16[1792,3584]{0,1:T(8,128)(2,1)} %bitcast.11) | data formatting | bytes 25690112
  351.1 138.0 %all-gather.8.cloned.1.call-done = bf16[1792,3584]{1,0:T(8,128)(2,1)} async-done(((bf16[1792,1792]{1,0:T(8,128)(2,1)}), bf16[1792,3584]{1,0:T(8,128)(2,1)}) %all-gather.8.cloned.1.call-update) | async-done | bytes 12845072 | tf_op jit(solution)/shard_map/all_gather | solution.py:39
  489.1 0.0 copy-start.1
  489.1 18.1 %copy.17 = bf16[3584,1792]{1,0:T(8,128)(2,1)} copy(bf16[3584,1792]{0,1:T(8,128)(2,1)} %bitcast.12) | data formatting | bytes 25690112
  507.2 0.0 copy-done.1
  (2 shorter events, 0.0 us)
Async XLA Ops:
  7.2 0.9 copy-start
  7.2 8.6 %copy-start.2 = (bf16[1792,64]{0,1:T(8,128)(2,1)S(1)}, bf16[1792,64]{0,1:T(8,128)(2,1)}, u32[]{:S(2)}) copy-start(bf16[1792,64]{0,1:T(8,128)(2,1)} %param.15) | copy-start | bytes 688132
  7.2 8.6 %copy-start.3 = (bf16[64,1792]{1,0:T(8,128)(2,1)S(1)}, bf16[64,1792]{1,0:T(8,128)(2,1)}, u32[]{:S(2)}) copy-start(bf16[64,1792]{1,0:T(8,128)(2,1)} %param.16) | copy-start | bytes 688132
  7.2 167.5 %all-gather.4.cloned.1.call-start = ((), (), s32[]{:S(2)}) async-start(), calls=%async_computation | async-start | bytes 19267584 | tf_op jit(solution)/shard_map/all_gather | solution.py:37
  15.7 7.7 %copy-start.4 = (bf16[1792,64]{0,1:T(8,128)(2,1)S(1)}, bf16[1792,64]{0,1:T(8,128)(2,1)}, u32[]{:S(2)}) copy-start(bf16[1792,64]{0,1:T(8,128)(2,1)} %param.18) | copy-start | bytes 688132
  15.7 7.8 %copy-start.5 = (bf16[64,1792]{1,0:T(8,128)(2,1)S(1)}, bf16[64,1792]{1,0:T(8,128)(2,1)}, u32[]{:S(2)}) copy-start(bf16[64,1792]{1,0:T(8,128)(2,1)} %param.19) | copy-start | bytes 688132
  15.7 316.4 %all-gather.6.cloned.1.call-start = ((), (), s32[]{:S(2)}) async-start(), calls=%async_computation.1 | async-start | bytes 19267584 | tf_op jit(solution)/shard_map/all_gather | solution.py:38
  23.4 9.6 %copy-start.8 = (u32[32]{0:T(128)S(1)}, u32[32]{0:T(128)}, u32[]{:S(2)}) copy-start(u32[32]{0:T(128)} %constant.2) | copy-start | bytes 388
  23.4 10.9 %copy-start.6 = (f32[224]{0:T(256)S(1)}, f32[224]{0:T(256)}, u32[]{:S(2)}) copy-start(f32[224]{0:T(256)} %param.20) | copy-start | bytes 2692
  23.4 10.9 %copy-start.7 = (f32[224]{0:T(256)S(1)}, f32[224]{0:T(256)}, u32[]{:S(2)}) copy-start(f32[224]{0:T(256)} %param.21) | copy-start | bytes 2692
  23.4 465.7 %all-gather.8.cloned.1.call-start = ((), (), s32[]{:S(2)}) async-start(), calls=%async_computation.2 | async-start | bytes 19267584 | tf_op jit(solution)/shard_map/all_gather | solution.py:39
  489.1 18.1 %copy-start.1 = (bf16[1792,64]{0,1:T(8,128)(2,1)S(1)}, bf16[1792,64]{0,1:T(8,128)(2,1)}, u32[]{:S(2)}) copy-start(bf16[1792,64]{0,1:T(8,128)(2,1)} %param.12) | copy-start | bytes 688132
Sparse Core Ops, SparseCore 0:
  15.8 158.7 all-gather.3
  176.8 155.2 all-gather.5
  333.7 155.3 all-gather.7
where the time goes:
time: 515 us; the launch traced here: 514 us
  waiting for transfers between devices  380 us (74%)
  local copies, waits for them, and re-layouts  57.8 us (11%)
  blocking collectives  36.7 us (7%)
  matrix products  24.6 us (5%)
  between operations  14.5 us (3%)
    all_gather x1, waiting for transfers between devices, local(): lax.all_gather(narrow_up, 'rows', axis=0, tiled=True)  138 us
    all_gather x1, waiting for transfers between devices, local(): lax.all_gather(narrow_down, 'rows', axis=1, tiled=True)  138 us
    all_gather x1, waiting for transfers between devices, local(): lax.all_gather(narrow_gate, 'rows', axis=0, tiled=True)  103 us
    unnamed x24, local copies, waits for them, and re-layouts  57.8 us
    unnamed x1, blocking collectives  36.7 us
  transfers between devices with their start and end apart: 3, of which 3 were waited for; matrix products, arithmetic and copies ran while one was open for 11% of the time, Pallas kernels for 0%

commit v1 on v0

v1 whole, which is shorter than its diff:
```python
import functools

import jax
import jax.numpy as jnp
from jax import lax
from jax.experimental import pallas as pl
from jax.experimental.pallas import tpu as pltpu
from jax.sharding import PartitionSpec as P


mix_rate = 1.0


def merge_body(train_ref, low_ref, high_ref, *rest):
    send_ref, out_ref = rest[-2:]
    whole = train_ref[...].astype(jnp.float32) + mix_rate * lax.dot_general(
        low_ref[...],
        high_ref[...],
        (((0,), (0,)), ((), ())),
        preferred_element_type=jnp.float32,
    )
    narrow = whole.astype(jnp.bfloat16)
    send_ref[...] = narrow
    out_ref[...] = narrow.T


def merge_chunk(train, low, high, out, before, out_shape, first, count, tile, place):
    width = train.shape[1]
    rank = low.shape[0]
    rows = count * tile
    in_specs = [
        pl.BlockSpec((tile, width), lambda i: (first + i, 0)),
        pl.BlockSpec((rank, tile), lambda i: (0, first + i)),
        pl.BlockSpec((rank, width), lambda i: (0, 0)),
    ]
    args = [train, low, high]
    aliases = {}
    if out is not None:
        in_specs.append(pl.BlockSpec(memory_space=pl.ANY))
        args.append(out)
        aliases = {3: 1}
    if before is not None:
        in_specs.append(pl.BlockSpec(memory_space=pl.ANY))
        args.append(before)
    return pl.pallas_call(
        merge_body,
        grid=(count,),
        in_specs=in_specs,
        out_specs=(
            pl.BlockSpec((tile, width), lambda i: (i, 0)),
            pl.BlockSpec((width, tile), lambda i: place(lax.axis_index("rows"), first + i)),
        ),
        out_shape=(
            jax.ShapeDtypeStruct((rows, width), jnp.bfloat16),
            jax.ShapeDtypeStruct(out_shape, jnp.bfloat16),
        ),
        input_output_aliases=aliases,
        compiler_params=pltpu.CompilerParams(vmem_limit_bytes=67_043_328),
        cost_estimate=pl.CostEstimate(
            flops=2 * rows * rank * width, bytes_accessed=6 * rows * width, transcendentals=0
        ),
    )(*args)


def turn_body(chunk_ref, *rest):
    out_ref = rest[-1]
    out_ref[...] = chunk_ref[...].T


def turn_chunk(chunk, out, before, first, shift, n, tile, place):
    rows, width = chunk.shape

    def where(i):
        source = lax.rem(lax.axis_index("rows") + (n - shift), n)
        return place(source, first + i)

    return pl.pallas_call(
        turn_body,
        grid=(rows // tile,),
        in_specs=[
            pl.BlockSpec((tile, width), lambda i: (i, 0)),
            pl.BlockSpec(memory_space=pl.ANY),
            pl.BlockSpec(memory_space=pl.ANY),
        ],
        out_specs=pl.BlockSpec((width, tile), where),
        out_shape=jax.ShapeDtypeStruct(out.shape, jnp.bfloat16),
        input_output_aliases={1: 0},
        compiler_params=pltpu.CompilerParams(vmem_limit_bytes=67_043_328),
        cost_estimate=pl.CostEstimate(
            flops=0, bytes_accessed=4 * rows * width, transcendentals=0
        ),
    )(chunk, out, before)


def tile_of(rows):
    return 256 if rows % 256 == 0 else 128


def send(chunk, n):
    return [
        lax.ppermute(chunk, "rows", [(d, (d + s) % n) for d in range(n)]) for s in range(1, n)
    ]


def local(
    n,
    train_gate,
    low_gate,
    high_gate,
    train_up,
    low_up,
    high_up,
    train_down,
    low_down,
    high_down,
    norm_train,
    norm_step,
):
    def side(train, low, high):
        rows, width = train.shape
        tile = tile_of(rows)
        tiles = rows // tile
        return train, low.T, high, (width, n * rows), lambda d, t: (0, d * tiles + t)

    def stack(train, low, high):
        rows, width = train.shape
        return train, low.T, high, (n * width, rows), lambda d, t: (d, t)

    matrices = (
        side(train_gate, low_gate, high_gate),
        side(train_up, low_up, high_up),
        stack(train_down, low_down, high_down),
    )
    outs = [None] * 3
    pending = []
    chunk = None
    for m, (train, low, high, shape, place) in enumerate(matrices):
        tile = tile_of(train.shape[0])
        tiles = train.shape[0] // tile
        if m == 0:
            counts = (1, tiles - 1)
        elif m == 1:
            counts = (tiles,)
        else:
            counts = (tiles - 1, 1)
        first = 0
        for count in counts:
            if count == 0:
                continue
            chunk, outs[m] = merge_chunk(
                train, low, high, outs[m], chunk, shape, first, count, tile, place
            )
            pending.append((m, first, tile, place, send(chunk, n)))
            first += count
    norm_train, norm_step, before = lax.optimization_barrier((norm_train, norm_step, chunk))
    serve_norm = lax.all_gather(
        (norm_train + norm_step).astype(jnp.bfloat16), ("rows", "cols"), axis=0, tiled=True
    )
    before, last = chunk, None
    for m, first, tile, place, arrivals in pending:
        for s, chunk in enumerate(arrivals, 1):
            if m == last:
                before = chunk
            outs[m] = before = turn_chunk(chunk, outs[m], before, first, s, n, tile, place)
            last = m
    return (*outs, serve_norm)


def plain(
    train_gate,
    low_gate,
    high_gate,
    train_up,
    low_up,
    high_up,
    train_down,
    low_down,
    high_down,
    norm_train,
    norm_step,
):
    def merged(train, low, high):
        whole = train.astype(jnp.float32) + mix_rate * jnp.dot(
            low, high, preferred_element_type=jnp.float32
        )
        return whole.astype(jnp.bfloat16)

    gather = functools.partial(lax.all_gather, axis_name="rows", tiled=True)
    return (
        gather(merged(train_gate, low_gate, high_gate), axis=0).T,
        gather(merged(train_up, low_up, high_up), axis=0).T,
        gather(merged(train_down, low_down, high_down), axis=1).T,
        lax.all_gather(
            (norm_train + norm_step).astype(jnp.bfloat16), ("rows", "cols"), axis=0, tiled=True
        ),
    )


def body(n, *args):
    sides = args[0].shape + args[3].shape + args[6].shape
    if any(side % 128 for side in sides):
        return plain(*args)
    return local(n, *args)


def solution(mesh):
    return jax.shard_map(
        functools.partial(body, mesh.shape["rows"]),
        mesh=mesh,
        in_specs=(
            P(("shift", "rows"), "cols"),
            P(("shift", "rows"), None),
            P("shift", "cols"),
            P(("shift", "rows"), "cols"),
            P(("shift", "rows"), None),
            P("shift", "cols"),
            P(("shift", "cols"), "rows"),
            P(("shift", "cols"), None),
            P("shift", "rows"),
            P(("shift", "rows", "cols")),
            P(("shift", "rows", "cols")),
        ),
        out_specs=(
            P(("shift", "cols"), None),
            P(("shift", "cols"), None),
            P("shift", "cols"),
            P("shift"),
        ),
        check_vma=False,
    )
```

time: 515 us -> 450 us (0.87)
  Pallas kernels: 0 us -> 60.9 us
  local copies, waits for them, and re-layouts: 57.8 us -> 1.45 us
  waiting for transfers between devices: 380 us -> 344 us
  matrix products: 24.6 us -> 0 us
  between operations: 14.5 us -> 1.29 us
  starting transfers between devices: 0.12 us -> 7.04 us
    all_gather x3 -> x0, waiting for transfers between devices: 380 us -> none  [the longest x1 138 us: local(): lax.all_gather(narrow_up, 'rows', axis=0, tiled=True)]
    ppermute x0 -> x5, waiting for transfers between devices: none -> 344 us  [send(): lax.ppermute(chunk, 'rows', [(d, (d + s) % n) for d in range(n)])]
    pallas_call x0 -> x10, Pallas kernels: none -> 60.9 us  [the longest x5 33.2 us: merge_chunk(): pl.pallas_call(merge_body, grid=(count,), in_specs=in_specs, out_specs=(p...]
    unnamed x24 -> x3, local copies, waits for them, and re-layouts: 57.8 us -> 1.45 us
    dot_general x3 -> x0, matrix products: 24.6 us -> none  [the longest x1 9.49 us: local(): jnp.dot(low_down, high_down, preferred_element_type=jnp.float32)]
    ppermute x0 -> x5, starting transfers between devices: none -> 7.04 us  [send(): lax.ppermute(chunk, 'rows', [(d, (d + s) % n) for d in range(n)])]
  transfers between devices with their start and end apart: 3 -> 5, of which waited for: 3 -> 1; matrix products, arithmetic and copies ran while one was open for 11% -> 0% of each run, Pallas kernels for 0% -> 8%
where the time goes in v1:
time: 450 us; the launch traced here: 449 us
  waiting for transfers between devices  344 us (76%)
  Pallas kernels  60.9 us (14%)
  blocking collectives  33 us (7%)
  starting transfers between devices  7.04 us (2%)
    ppermute x5, waiting for transfers between devices, send(): lax.ppermute(chunk, 'rows', [(d, (d + s) % n) for d in range(n)])  344 us
    pallas_call x5, Pallas kernels, merge_chunk(): pl.pallas_call(merge_body, grid=(count,), in_specs=in_specs, out_specs=(p...  33.2 us
    unnamed x1, blocking collectives  33 us
    pallas_call x5, Pallas kernels, turn_chunk(): pl.pallas_call(turn_body, grid=(rows // tile,), in_specs=[pl.BlockSpec((t...  27.6 us
  transfers between devices with their start and end apart: 5, of which 1 were waited for; matrix products, arithmetic and copies ran while one was open for 0% of the time, Pallas kernels for 8%

profile of v1, /device:TPU:0, one launch (start us, length us, event | category | flops | bytes accessed | tf_op | source)
XLA Modules:
  0.0 448.8 jit_solution(14211569066028309444)
XLA Ops:
  0.6 2.9 shard_map.138
  3.5 8.6 %shard_map.139 = (bf16[1536,1792]{1,0:T(8,128)(2,1)}, bf16[1792,3584]{1,0:T(8,128)(2,1)}) custom-call(bf16[1792,1792]{1,0:T(8,128)(2,1)} %train_ref.6, bf16[64,1792]{1,0:T(8,128)(2,1)} %bitcast.7, bf16[64,1792]{1,0:T(8,128)(2,1)} %high_ref.6, bf16[1792,3584]{1,0:T(8,128)(2,1)} %get-tuple-element.16.rest_0_, ...), custom_call_target="tpu_custom_call", output_to_operand_aliasing={{1}: (3, {})} | custom-call | flops 352321536 | bytes 16515072 | tf_op jit(solution)/shard_map/pallas_call | solution.py:45
  12.1 10.2 %shard_map.140 = (bf16[1792,1792]{1,0:T(8,128)(2,1)}, bf16[1792,3584]{1,0:T(8,128)(2,1)}) custom-call(bf16[1792,1792]{1,0:T(8,128)(2,1)} %train_ref.7, bf16[64,1792]{1,0:T(8,128)(2,1)} %bitcast.8, bf16[64,1792]{1,0:T(8,128)(2,1)} %high_ref.7, bf16[1536,1792]{1,0:T(8,128)(2,1)} %get-tuple-element.18.rest_0_), custom_call_target="tpu_custom_call" | custom-call | flops 411041792 | bytes 19267584 | tf_op jit(solution)/shard_map/pallas_call | solution.py:45
  22.4 3.0 collective-permute-start.2
  25.4 0.0 collective-permute-start
  25.4 8.6 %shard_map.141 = (bf16[1536,1792]{1,0:T(8,128)(2,1)}, bf16[3584,1792]{1,0:T(8,128)(2,1)}) custom-call(bf16[1792,1792]{1,0:T(8,128)(2,1)} %train_ref.9, bf16[64,1792]{1,0:T(8,128)(2,1)} %bitcast.4, bf16[64,1792]{1,0:T(8,128)(2,1)} %high_ref.9, bf16[1792,1792]{1,0:T(8,128)(2,1)} %get-tuple-element.20.rest_0_), custom_call_target="tpu_custom_call" | custom-call | flops 352321536 | bytes 16515072 | tf_op jit(solution)/shard_map/pallas_call | solution.py:45
  34.0 2.0 collective-permute-start.4
  36.0 0.0 collective-permute-start.1
  36.0 2.9 shard_map.142
  38.9 2.0 collective-permute-start.3
  40.9 1.2 dynamic-slice
  42.8 0.7 add_convert_fusion
  43.5 0.2 dynamic-update-slice
  43.7 33.0 %all-reduce = bf16[3584]{0:T(1024)(128)(2,1)} all-reduce(bf16[3584]{0:T(1024)(128)(2,1)S(1)} %dynamic-update-slice), channel_id=1, replica_groups=mesh['rows'=2,'cols'=8,'shift'=2] {'rows','cols'}, use_global_device_ids=true, to_apply=%add | all-reduce | flops 3584 | bytes 14336
  76.7 344.5 %collective-permute-done.1.chunk_ref = bf16[256,1792]{1,0:T(8,128)(2,1)} collective-permute-done((bf16[256,1792]{1,0:T(8,128)(2,1)}, bf16[256,1792]{1,0:T(8,128)(2,1)}, u32[]{:S(2)}, u32[]{:S(2)}) %collective-permute-start.1) | collective-permute-done | bytes 917536 | tf_op jit(solution)/shard_map/ppermute | solution.py:101
  421.2 2.4 shard_map.143.rest_0_
  423.5 0.0 collective-permute-done.chunk_ref.rest_1_
  423.6 7.0 %shard_map.144.rest_1_ = bf16[1792,3584]{1,0:T(8,128)(2,1)} custom-call(bf16[1536,1792]{1,0:T(8,128)(2,1)} %collective-permute-done.chunk_ref.rest_1_, bf16[1792,3584]{1,0:T(8,128)(2,1)} %shard_map.143.rest_0_, bf16[1536,1792]{1,0:T(8,128)(2,1)} %collective-permute-done.chunk_ref.rest_1_), custom_call_target="tpu_custom_call", output_to_operand_aliasing={{}: (1, {})} | custom-call | bytes 11010048 | tf_op jit(solution)/shard_map/pallas_call | solution.py:77
  430.6 0.0 collective-permute-done.2.chunk_ref
  430.6 8.8 %shard_map.145.rest_1_ = bf16[1792,3584]{1,0:T(8,128)(2,1)} custom-call(bf16[1792,1792]{1,0:T(8,128)(2,1)} %collective-permute-done.2.chunk_ref, bf16[1792,3584]{1,0:T(8,128)(2,1)} %get-tuple-element.24.rest_0_, bf16[1792,3584]{1,0:T(8,128)(2,1)} %shard_map.144.rest_1_), custom_call_target="tpu_custom_call", output_to_operand_aliasing={{}: (1, {})} | custom-call | bytes 12845056 | tf_op jit(solution)/shard_map/pallas_call | solution.py:77
  439.4 0.0 collective-permute-done.4.chunk_ref
  439.4 7.0 %shard_map.146.rest_0_ = bf16[3584,1792]{1,0:T(8,128)(2,1)} custom-call(bf16[1536,1792]{1,0:T(8,128)(2,1)} %collective-permute-done.4.chunk_ref, bf16[3584,1792]{1,0:T(8,128)(2,1)} %get-tuple-element.25.rest_0_, bf16[1792,3584]{1,0:T(8,128)(2,1)} %shard_map.145.rest_1_), custom_call_target="tpu_custom_call", output_to_operand_aliasing={{}: (1, {})} | custom-call | bytes 11010048 | tf_op jit(solution)/shard_map/pallas_call | solution.py:77
  446.4 0.0 collective-permute-done.3.chunk_ref.rest_1_
  446.4 2.4 shard_map.147
  (1 shorter events, 0.0 us)
Async XLA Ops:
  22.4 408.2 %collective-permute-start.2 = (bf16[1792,1792]{1,0:T(8,128)(2,1)}, bf16[1792,1792]{1,0:T(8,128)(2,1)}, u32[]{:S(2)}, u32[]{:S(2)}) collective-permute-start(bf16[1792,1792]{1,0:T(8,128)(2,1)} %get-tuple-element.20.rest_0_), channel_id=1, source_target_pairs={{0,16},{16,0},{1,17},{17,1},{2,18},{18,2},{3,19},{19,3},{4,20},{20... | collective-permute-start | bytes 19267592 | tf_op jit(solution)/shard_map/ppermute | solution.py:101
  25.4 398.2 %collective-permute-start = (bf16[1536,1792]{1,0:T(8,128)(2,1)}, bf16[1536,1792]{1,0:T(8,128)(2,1)}, u32[]{:S(2)}, u32[]{:S(2)}) collective-permute-start(bf16[1536,1792]{1,0:T(8,128)(2,1)} %get-tuple-element.18.rest_0_), channel_id=1, source_target_pairs={{0,16},{16,0},{1,17},{17,1},{2,18},{18,2},{3,19},{19,3},{4,20},{20... | collective-permute-start | bytes 16515080 | tf_op jit(solution)/shard_map/ppermute | solution.py:101
  34.0 405.4 %collective-permute-start.4 = (bf16[1536,1792]{1,0:T(8,128)(2,1)}, bf16[1536,1792]{1,0:T(8,128)(2,1)}, u32[]{:S(2)}, u32[]{:S(2)}) collective-permute-start(bf16[1536,1792]{1,0:T(8,128)(2,1)} %get-tuple-element.22.rest_1_), channel_id=1, source_target_pairs={{0,16},{16,0},{1,17},{17,1},{2,18},{18,2},{3,19},{19,3},{4,20},{20... | collective-permute-start | bytes 16515080 | tf_op jit(solution)/shard_map/ppermute | solution.py:101
  36.0 385.2 %collective-permute-start.1 = (bf16[256,1792]{1,0:T(8,128)(2,1)}, bf16[256,1792]{1,0:T(8,128)(2,1)}, u32[]{:S(2)}, u32[]{:S(2)}) collective-permute-start(bf16[256,1792]{1,0:T(8,128)(2,1)} %get-tuple-element.17.rest_1_), channel_id=1, source_target_pairs={{0,16},{16,0},{1,17},{17,1},{2,18},{18,2},{3,19},{19,3},{4,20},{20... | collective-permute-start | bytes 2752520 | tf_op jit(solution)/shard_map/ppermute | solution.py:101
  38.9 407.5 %collective-permute-start.3 = (bf16[256,1792]{1,0:T(8,128)(2,1)}, bf16[256,1792]{1,0:T(8,128)(2,1)}, u32[]{:S(2)}, u32[]{:S(2)}) collective-permute-start(bf16[256,1792]{1,0:T(8,128)(2,1)} %get-tuple-element.23.rest_1_), channel_id=1, source_target_pairs={{0,16},{16,0},{1,17},{17,1},{2,18},{18,2},{3,19},{19,3},{4,20},{20... | collective-permute-start | bytes 2752520 | tf_op jit(solution)/shard_map/ppermute | solution.py:101

commit v2 on v1

--- a/solution.py
+++ b/solution.py
@@ -9,19 +9,48 @@
 
 
 mix_rate = 1.0
-
-
-def merge_body(train_ref, low_ref, high_ref, *rest):
-    send_ref, out_ref = rest[-2:]
+TILE = 128
+
+
+def merged(train_ref, low_ref, high_ref):
     whole = train_ref[...].astype(jnp.float32) + mix_rate * lax.dot_general(
         low_ref[...],
         high_ref[...],
         (((0,), (0,)), ((), ())),
         preferred_element_type=jnp.float32,
     )
-    narrow = whole.astype(jnp.bfloat16)
+    return whole.astype(jnp.bfloat16)
+
+
+def merge_body(train_ref, low_ref, high_ref, *rest):
+    send_ref, out_ref = rest[-2:]
+    narrow = merged(train_ref, low_ref, high_ref)
     send_ref[...] = narrow
     out_ref[...] = narrow.T
+
+
+def head_body(train_ref, low_ref, high_ref, send_ref):
+    send_ref[...] = merged(train_ref, low_ref, high_ref)
+
+
+def head_chunk(train, low, high, tile):
+    width = train.shape[1]
+    rank = low.shape[0]
+    return pl.pallas_call(
+        head_body,
+        grid=(1,),
+        in_specs=[
+            pl.BlockSpec((tile, width), lambda i: (0, 0)),
+            pl.BlockSpec((rank, tile), lambda i: (0, 0)),
+            pl.BlockSpec((rank, width), lambda i: (0, 0)),
+        ],
+        out_specs=pl.BlockSpec((tile, width), lambda i: (0, 0)),
+        out_shape=jax.ShapeDtypeStruct((tile, width), jnp.bfloat16),
+        compiler_params=pltpu.CompilerParams(vmem_limit_bytes=67_043_328),
+        cost_estimate=pl.CostEstimate(
+            flops=2 * tile * rank * width, bytes_accessed=4 * tile * width, transcendentals=0
+        ),
+    )(train, low, high)
 
 
 def merge_chunk(train, low, high, out, before, out_shape, first, count, tile, place):
@@ -67,11 +96,12 @@
     out_ref[...] = chunk_ref[...].T
 
 
-def turn_chunk(chunk, out, before, first, shift, n, tile, place):
+def turn_chunk(chunk, out, before, first, shift, n, tile, place, vmem=64_000_000):
     rows, width = chunk.shape
+    args = (chunk, out) if before is None else (chunk, out, before)
 
     def where(i):
-        source = lax.rem(lax.axis_index("rows") + (n - shift), n)
+        source = lax.rem(lax.axis_index("rows") + n - shift, n)
         return place(source, first + i)
 
     return pl.pallas_call(
@@ -79,21 +109,16 @@
         grid=(rows // tile,),
         in_specs=[
             pl.BlockSpec((tile, width), lambda i: (i, 0)),
-            pl.BlockSpec(memory_space=pl.ANY),
-            pl.BlockSpec(memory_space=pl.ANY),
+            *[pl.BlockSpec(memory_space=pl.ANY)] * (len(args) - 1),
         ],
         out_specs=pl.BlockSpec((width, tile), where),
         out_shape=jax.ShapeDtypeStruct(out.shape, jnp.bfloat16),
         input_output_aliases={1: 0},
-        compiler_params=pltpu.CompilerParams(vmem_limit_bytes=67_043_328),
+        compiler_params=pltpu.CompilerParams(vmem_limit_bytes=vmem),
         cost_estimate=pl.CostEstimate(
             flops=0, bytes_accessed=4 * rows * width, transcendentals=0
         ),
-    )(chunk, out, before)
-
-
-def tile_of(rows):
-    return 256 if rows % 256 == 0 else 128
+    )(*args)
 
 
 def send(chunk, n):
@@ -116,9 +141,10 @@
     norm_train,
     norm_step,
 ):
+    tile = TILE
+
     def side(train, low, high):
         rows, width = train.shape
-        tile = tile_of(rows)
         tiles = rows // tile
         return train, low.T, high, (width, n * rows), lambda d, t: (0, d * tiles + t)
 
@@ -133,36 +159,38 @@
     )
     outs = [None] * 3
     pending = []
-    chunk = None
+    chunk = head = None
     for m, (train, low, high, shape, place) in enumerate(matrices):
-        tile = tile_of(train.shape[0])
         tiles = train.shape[0] // tile
         if m == 0:
-            counts = (1, tiles - 1)
+            cuts = (0, 1, 1 + (tiles - 1) // 3, tiles)
         elif m == 1:
-            counts = (tiles,)
+            cuts = (0, tiles)
         else:
-            counts = (tiles - 1, 1)
-        first = 0
-        for count in counts:
-            if count == 0:
+            cuts = (0, max(tiles - 3, 0), max(tiles - 1, 0), tiles)
+        for first, end in zip(cuts, cuts[1:]):
+            if first == end:
                 continue
-            chunk, outs[m] = merge_chunk(
-                train, low, high, outs[m], chunk, shape, first, count, tile, place
-            )
-            pending.append((m, first, tile, place, send(chunk, n)))
-            first += count
+            k = len(pending)
+            if k == 0:
+                chunk = head = head_chunk(train, low, high, tile)
+            else:
+                chunk, outs[m] = merge_chunk(
+                    train, low, high, outs[m], chunk, shape, first, end - first, tile, place
+                )
+            pending.append((m, first, place, send(chunk, n)))
     norm_train, norm_step, before = lax.optimization_barrier((norm_train, norm_step, chunk))
     serve_norm = lax.all_gather(
         (norm_train + norm_step).astype(jnp.bfloat16), ("rows", "cols"), axis=0, tiled=True
     )
-    before, last = chunk, None
-    for m, first, tile, place, arrivals in pending:
+    outs[0] = turn_chunk(head, outs[0], chunk, 0, 0, n, tile, matrices[0][4])
+    last = 0
+    for k, (m, first, place, arrivals) in enumerate(pending):
+        vmem = 32_000_000 if k == len(pending) - 1 else 64_000_000
+        before = None if m == last else outs[last]
         for s, chunk in enumerate(arrivals, 1):
-            if m == last:
-                before = chunk
-            outs[m] = before = turn_chunk(chunk, outs[m], before, first, s, n, tile, place)
-            last = m
+            outs[m] = turn_chunk(chunk, outs[m], before, first, s, n, tile, place, vmem)
+            before, last = None, m
     return (*outs, serve_norm)
 
 

time: 450 us -> 498 us (1.11)
  Pallas kernels: 60.9 us -> 84.2 us
  waiting for transfers between devices: 344 us -> 367 us
    ppermute x5 -> x7, waiting for transfers between devices: 344 us -> 367 us  [send(): lax.ppermute(chunk, 'rows', [(d, (d + s) % n) for d in range(n)])]
    pallas_call x5 -> x8, Pallas kernels: 27.6 us -> 38.9 us  [turn_chunk(): pl.pallas_call(turn_body, grid=(rows // tile,), in_specs=[pl.BlockSpec((t...]
    pallas_call x5 -> x6, Pallas kernels: 33.2 us -> 43.1 us  [merge_chunk(): pl.pallas_call(merge_body, grid=(count,), in_specs=in_specs, out_specs=(p...]
  transfers between devices with their start and end apart: 5 -> 7, of which waited for: 1 -> 1; matrix products, arithmetic and copies ran while one was open for 0% -> 0% of each run, Pallas kernels for 8% -> 11%
where the time goes in v2:
time: 498 us; the launch traced here: 496 us
  waiting for transfers between devices  367 us (74%)
  Pallas kernels  84.2 us (17%)
  blocking collectives  33.9 us (7%)
  starting transfers between devices  9.09 us (2%)
    ppermute x7, waiting for transfers between devices, send(): lax.ppermute(chunk, 'rows', [(d, (d + s) % n) for d in range(n)])  367 us
    pallas_call x6, Pallas kernels, merge_chunk(): pl.pallas_call(merge_body, grid=(count,), in_specs=in_specs, out_specs=(p...  43.1 us
    pallas_call x8, Pallas kernels, turn_chunk(): pl.pallas_call(turn_body, grid=(rows // tile,), in_specs=[pl.BlockSpec((t...  38.9 us
    unnamed x1, blocking collectives  33.9 us
  transfers between devices with their start and end apart: 7, of which 1 were waited for; matrix products, arithmetic and copies ran while one was open for 0% of the time, Pallas kernels for 11%

profile of v2, /device:TPU:0, one launch (start us, length us, event | category | flops | bytes accessed | tf_op | source)
XLA Modules:
  0.0 496.0 jit_solution(4155238392196407252)
XLA Ops:
  0.6 2.2 shard_map.138.rest_0_.chunk_ref
  2.8 4.6 shard_map.139
  7.4 9.3 %shard_map.140 = (bf16[1152,1792]{1,0:T(8,128)(2,1)}, bf16[1792,3584]{1,0:T(8,128)(2,1)}) custom-call(bf16[1792,1792]{1,0:T(8,128)(2,1)} %train_ref.9, bf16[64,1792]{1,0:T(8,128)(2,1)} %bitcast.9, bf16[64,1792]{1,0:T(8,128)(2,1)} %high_ref.9, bf16[1792,3584]{1,0:T(8,128)(2,1)} %get-tuple-element.18.rest_0_, ...), custom_call_target="tpu_custom_call", output_to_operand_aliasing={{1}: (3, {})} | custom-call | flops 264241152 | bytes 12386304 | tf_op jit(solution)/shard_map/pallas_call | solution.py:74
  16.7 13.3 %shard_map.141 = (bf16[1792,1792]{1,0:T(8,128)(2,1)}, bf16[1792,3584]{1,0:T(8,128)(2,1)}) custom-call(bf16[1792,1792]{1,0:T(8,128)(2,1)} %train_ref.10, bf16[64,1792]{1,0:T(8,128)(2,1)} %bitcast.10, bf16[64,1792]{1,0:T(8,128)(2,1)} %high_ref.10, bf16[1152,1792]{1,0:T(8,128)(2,1)} %get-tuple-element.20.rest_0_), custom_call_target="tpu_custom_call" | custom-call | flops 411041792 | bytes 19267584 | tf_op jit(solution)/shard_map/pallas_call | solution.py:74
  29.9 3.0 collective-permute-start.3
  32.9 10.9 %shard_map.142 = (bf16[1408,1792]{1,0:T(8,128)(2,1)}, bf16[3584,1792]{1,0:T(8,128)(2,1)}) custom-call(bf16[1792,1792]{1,0:T(8,128)(2,1)} %train_ref.13, bf16[64,1792]{1,0:T(8,128)(2,1)} %bitcast.4, bf16[64,1792]{1,0:T(8,128)(2,1)} %high_ref.13, bf16[1792,1792]{1,0:T(8,128)(2,1)} %get-tuple-element.22.rest_0_), custom_call_target="tpu_custom_call" | custom-call | flops 322961408 | bytes 15138816 | tf_op jit(solution)/shard_map/pallas_call | solution.py:74
  43.9 0.0 collective-permute-start.6
  43.9 2.0 collective-permute-start
  45.9 0.0 collective-permute-start.1
  45.9 2.0 collective-permute-start.2
  47.9 2.8 shard_map.143
  50.7 366.7 %collective-permute-done.2.chunk_ref = bf16[128,1792]{1,0:T(8,128)(2,1)} collective-permute-done((bf16[128,1792]{1,0:T(8,128)(2,1)}, bf16[128,1792]{1,0:T(8,128)(2,1)}, u32[]{:S(2)}, u32[]{:S(2)}) %collective-permute-start.2) | collective-permute-done | bytes 458784 | tf_op jit(solution)/shard_map/ppermute | solution.py:126
  417.3 1.7 collective-permute-start.5
  419.1 2.3 shard_map.144
  421.4 0.0 collective-permute-done.1.chunk_ref
  421.4 0.3 collective-permute-start.4
  421.7 0.0 copy-start.2
  421.7 0.0 copy-start
  421.7 0.0 copy-start.1
  421.7 2.0 shard_map.145.rest_0_
  423.7 0.0 copy-done.2
  423.7 0.6 dynamic-slice
  424.9 0.0 copy-done
  424.9 0.0 copy-done.1
  425.0 0.2 dynamic-update-slice
  425.2 33.9 %all-reduce = bf16[3584]{0:T(1024)(128)(2,1)} all-reduce(bf16[3584]{0:T(1024)(128)(2,1)S(1)} %dynamic-update-slice), channel_id=1, replica_groups=mesh['rows'=2,'cols'=8,'shift'=2] {'rows','cols'}, use_global_device_ids=true, to_apply=%add | all-reduce | flops 3584 | bytes 14336
  459.1 2.0 shard_map.146.rest_0_
  461.1 3.9 shard_map.147.rest_0_
  465.0 0.0 collective-permute-done.chunk_ref
  465.0 7.7 %shard_map.148.rest_1_ = bf16[1792,3584]{1,0:T(8,128)(2,1)} custom-call(bf16[1152,1792]{1,0:T(8,128)(2,1)} %collective-permute-done.chunk_ref, bf16[1792,3584]{1,0:T(8,128)(2,1)} %shard_map.147.rest_0_), custom_call_target="tpu_custom_call", output_to_operand_aliasing={{}: (1, {})} | custom-call | bytes 8257536 | tf_op jit(solution)/shard_map/pallas_call | solution.py:107
  472.7 0.0 collective-permute-done.3.chunk_ref
  472.7 11.1 %shard_map.149.rest_1_ = bf16[1792,3584]{1,0:T(8,128)(2,1)} custom-call(bf16[1792,1792]{1,0:T(8,128)(2,1)} %collective-permute-done.3.chunk_ref, bf16[1792,3584]{1,0:T(8,128)(2,1)} %get-tuple-element.28.rest_0_, bf16[1792,3584]{1,0:T(8,128)(2,1)} %shard_map.148.rest_1_), custom_call_target="tpu_custom_call", output_to_operand_aliasing={{}: (1, {})} | custom-call | bytes 12845056 | tf_op jit(solution)/shard_map/pallas_call | solution.py:107
  483.8 0.0 collective-permute-done.6.chunk_ref
  483.8 9.1 %shard_map.150.rest_0_ = bf16[3584,1792]{1,0:T(8,128)(2,1)} custom-call(bf16[1408,1792]{1,0:T(8,128)(2,1)} %collective-permute-done.6.chunk_ref, bf16[3584,1792]{1,0:T(8,128)(2,1)} %get-tuple-element.29.rest_0_, bf16[1792,3584]{1,0:T(8,128)(2,1)} %shard_map.149.rest_1_), custom_call_target="tpu_custom_call", output_to_operand_aliasing={{}: (1, {})} | custom-call | bytes 10092544 | tf_op jit(solution)/shard_map/pallas_call | solution.py:107
  492.9 0.0 collective-permute-done.5.chunk_ref
  492.9 2.1 shard_map.151.rest_0_
  495.1 0.0 collective-permute-done.4.chunk_ref
  495.1 0.9 shard_map.152
  (2 shorter events, 0.0 us)
Async XLA Ops:
  29.9 442.8 %collective-permute-start.3 = (bf16[1792,1792]{1,0:T(8,128)(2,1)}, bf16[1792,1792]{1,0:T(8,128)(2,1)}, u32[]{:S(2)}, u32[]{:S(2)}) collective-permute-start(bf16[1792,1792]{1,0:T(8,128)(2,1)} %get-tuple-element.22.rest_0_), channel_id=1, source_target_pairs={{0,16},{16,0},{1,17},{17,1},{2,18},{18,2},{3,19},{19,3},{4,20},{20... | collective-permute-start | bytes 19267592 | tf_op jit(solution)/shard_map/ppermute | solution.py:126
  43.9 440.0 %collective-permute-start.6 = (bf16[1408,1792]{1,0:T(8,128)(2,1)}, bf16[1408,1792]{1,0:T(8,128)(2,1)}, u32[]{:S(2)}, u32[]{:S(2)}) collective-permute-start(bf16[1408,1792]{1,0:T(8,128)(2,1)} %get-tuple-element.24.rest_1_), channel_id=1, source_target_pairs={{0,16},{16,0},{1,17},{17,1},{2,18},{18,2},{3,19},{19,3},{4,20},{20... | collective-permute-start | bytes 15138824 | tf_op jit(solution)/shard_map/ppermute | solution.py:126
  43.9 421.1 %collective-permute-start = (bf16[1152,1792]{1,0:T(8,128)(2,1)}, bf16[1152,1792]{1,0:T(8,128)(2,1)}, u32[]{:S(2)}, u32[]{:S(2)}) collective-permute-start(bf16[1152,1792]{1,0:T(8,128)(2,1)} %get-tuple-element.20.rest_0_), channel_id=1, source_target_pairs={{0,16},{16,0},{1,17},{17,1},{2,18},{18,2},{3,19},{19,3},{4,20},{20... | collective-permute-start | bytes 12386312 | tf_op jit(solution)/shard_map/ppermute | solution.py:126
  45.9 375.5 %collective-permute-start.1 = (bf16[512,1792]{1,0:T(8,128)(2,1)}, bf16[512,1792]{1,0:T(8,128)(2,1)}, u32[]{:S(2)}, u32[]{:S(2)}) collective-permute-start(bf16[512,1792]{1,0:T(8,128)(2,1)} %get-tuple-element.19.rest_1_), channel_id=1, source_target_pairs={{0,16},{16,0},{1,17},{17,1},{2,18},{18,2},{3,19},{19,3},{4,20},{20... | collective-permute-start | bytes 5505032 | tf_op jit(solution)/shard_map/ppermute | solution.py:126
  45.9 371.4 %collective-permute-start.2 = (bf16[128,1792]{1,0:T(8,128)(2,1)}, bf16[128,1792]{1,0:T(8,128)(2,1)}, u32[]{:S(2)}, u32[]{:S(2)}) collective-permute-start(bf16[128,1792]{1,0:T(8,128)(2,1)} %shard_map.138.rest_0_.chunk_ref), channel_id=1, source_target_pairs={{0,16},{16,0},{1,17},{17,1},{2,18},{18,2},{3,19},{19,3},{4,20},{20... | collective-permute-start | bytes 1376264 | tf_op jit(solution)/shard_map/ppermute | solution.py:126
  417.3 75.6 %collective-permute-start.5 = (bf16[256,1792]{1,0:T(8,128)(2,1)}, bf16[256,1792]{1,0:T(8,128)(2,1)}, u32[]{:S(2)}, u32[]{:S(2)}) collective-permute-start(bf16[256,1792]{1,0:T(8,128)(2,1)} %get-tuple-element.26.rest_1_), channel_id=1, source_target_pairs={{0,16},{16,0},{1,17},{17,1},{2,18},{18,2},{3,19},{19,3},{4,20},{20... | collective-permute-start | bytes 2752520 | tf_op jit(solution)/shard_map/ppermute | solution.py:126
  421.4 73.7 %collective-permute-start.4 = (bf16[128,1792]{1,0:T(8,128)(2,1)}, bf16[128,1792]{1,0:T(8,128)(2,1)S(1)}, u32[]{:S(2)}, u32[]{:S(2)}) collective-permute-start(bf16[128,1792]{1,0:T(8,128)(2,1)} %get-tuple-element.27.rest_1_), channel_id=1, source_target_pairs={{0,16},{16,0},{1,17},{17,1},{2,18},{18,2},{3,19},{19,3},{4,20},{20... | collective-permute-start | bytes 1376264 | tf_op jit(solution)/shard_map/ppermute | solution.py:126
  421.7 2.0 copy-start.2
  421.7 3.2 copy-start
  421.7 3.2 copy-start.1
